TPU v7x, 32 devices: a whole 2x2x4 slice. The times are simulated.
32 devices in a mesh: expert: 16 (over z, y, x), dp: 2 (over core).
Axes of the slice: x: 2, y: 2, z: 4, core: 2. Of those that a mesh axis runs over, the one named last changes fastest.
Arguments:
- patches: bfloat16 [512, 196, 1024], P(('dp', 'expert')), parts along dimension 0, may hold values from -6 to 6
- visible: int32 [512, 49], P(('dp', 'expert')), parts along dimension 0, may hold values from 0 to 195, as said below
- routes: int32 [25088, 1], P(('dp', 'expert')), parts along dimension 0, may hold values from 0 to 15; in each aligned block of 784 rows (0 to 783, 784 to 1567, ...) at most 74 rows name the same one
- expert_cap: int32 [32], P('dp'), parts along dimension 0, may hold values from 36 to 74
- norm_gain: float32 [1024], replicated, may hold values from 0.5 to 2
- norm_bias: float32 [1024], replicated, may hold values from -6 to 6
- router: float32 [1024, 16], replicated, may hold values from -0.1875 to 0.1875
- w_in: bfloat16 [16, 1024, 4096], P('expert'), may hold values from -0.1875 to 0.1875
- b_in: float32 [16, 4096], P('expert'), may hold values from -6 to 6
- w_out: bfloat16 [16, 4096, 1024], P('expert'), may hold values from -0.09375 to 0.09375
- b_out: float32 [16, 1024], P('expert'), may hold values from -6 to 6
Outputs:
- layer_out: bfloat16 [25088, 1024], P(('dp', 'expert')), parts along dimension 0
There are 2 independent parts, one for each index of `dp`. A program takes and returns all parts, laid end to end along the dimension named above; an argument that names none is the same for every part. Nothing has to cross between parts.
Inputs may be any that keep to these rules, and one draw needn't show every extreme that they name: `visible`: each row holds 49 different patch indices in increasing order. `routes`: among the tokens of one index of expert no expert is named more than 74 times.
All inputs are finite; a program needn't handle non-finite values.
Results may differ from a plain program's by a relative error of at most 0.005.
Values may be sent and summed in bfloat16 or wider, within the bound.
A program may use at most 128 MiB of HBM per device.

v0:
```python
import jax
import jax.numpy as jnp
from jax import lax
from jax.sharding import PartitionSpec as P


def expert_rows(rows, w_in, b_in, w_out, b_out):
    act = jax.nn.gelu(
        jnp.dot(rows, w_in[0], preferred_element_type=jnp.float32) + b_in[0], approximate=True
    ).astype(jnp.bfloat16)
    return (jnp.dot(act, w_out[0], preferred_element_type=jnp.float32) + b_out[0]).astype(
        jnp.bfloat16
    )


def send_back(result):
    return lax.all_to_all(result, "expert", split_axis=0, concat_axis=0, tiled=True)


def per_device(
    patches, visible, routes, expert_cap, norm_gain, norm_bias, router, w_in, b_in, w_out, b_out
):
    width = patches.shape[2]
    devices = lax.axis_size("expert")
    experts = expert_cap.shape[0]
    x = jnp.take_along_axis(patches, visible[:, :, None], axis=1).reshape(-1, width)
    tok_count = x.shape[0]
    slots = max(2, (3 * tok_count + 2 * experts - 1) // (2 * experts))
    xf = x.astype(jnp.float32)
    mean = jnp.mean(xf, axis=1, keepdims=True)
    var = jnp.mean((xf - mean) ** 2, axis=1, keepdims=True)
    h = (xf - mean) / jnp.sqrt(var + 1e-06) * norm_gain + norm_bias
    hb = h.astype(jnp.bfloat16)
    chosen = routes[:, 0]
    onehot = (chosen[:, None] == jnp.arange(experts, dtype=jnp.int32)[None, :]).astype(jnp.int32)
    logits = jnp.dot(h, router, precision=lax.Precision.HIGHEST)
    gate = jax.nn.sigmoid(jnp.sum(logits * onehot.astype(jnp.float32), axis=1))
    rank = jnp.sum((jnp.cumsum(onehot, axis=0) - onehot) * onehot, axis=1)
    limit = jnp.sum(onehot * expert_cap[None, :], axis=1)
    kept = rank < limit
    dest = jnp.where(kept, chosen * slots + rank, experts * slots)
    outgoing = (
        jnp.zeros((experts * slots + 1, width), jnp.bfloat16)
        .at[dest]
        .set(hb)[:-1]
        .reshape(experts, slots, width)
    )
    received = lax.all_to_all(outgoing, "expert", split_axis=0, concat_axis=0, tiled=True)
    count = received.shape[1]
    result = expert_rows(received.reshape(-1, width), w_in, b_in, w_out, b_out)
    back = send_back(result.reshape(devices, count, width))
    flat = back.reshape(experts * slots, width)
    picked = flat[jnp.minimum(dest, experts * slots - 1)].astype(jnp.float32)
    branch = jnp.where(kept[:, None], gate[:, None] * picked, 0.0)
    return (xf + branch).astype(jnp.bfloat16)


def solution(mesh):
    return jax.shard_map(
        per_device,
        mesh=mesh,
        in_specs=(
            P(("dp", "expert"), None, None),
            P(("dp", "expert"), None),
            P(("dp", "expert"), None),
            P("dp"),
            P(),
            P(),
            P(),
            P("expert", None, None),
            P("expert", None),
            P("expert", None, None),
            P("expert", None),
        ),
        out_specs=P(("dp", "expert"), None),
        check_vma=False,
    )
```

profile of v0, /device:TPU:12, one launch (start us, length us, event | category | flops | bytes accessed | tf_op | source)
XLA Modules:
  0.0 216.2 jit_solution(16963729803809097578)
XLA Ops:
  0.0 0.0 copy-start
  0.0 0.7 compare_and_fusion
  0.7 0.7 bitcast_or_fusion
  1.4 0.1 broadcast_in_dim.44
  1.5 0.1 reshape.116
  1.6 15.0 %gather_fusion.1 = bf16[784,1024]{1,0:T(8,128)(2,1)S(1)} fusion(bf16[16,196,1024]{2,0,1:T(8,128)(2,1)} %param.11, s32[784]{0:T(1024)S(1)} %reshape.116), kind=kCustom, calls=%fused_computation.1 | custom fusion | bytes 3217536 | tf_op jit(solution)/shard_map/jit(take_along_axis)/gather | solution.py:26
  16.6 0.0 copy-start.1
  16.6 0.0 copy-start.2
  16.7 0.0 copy-start.5
  16.7 0.0 copy-start.3
  16.7 0.0 copy-start.4
  16.7 0.6 reshape.119
  17.3 0.6 convert_reduce_fusion
  17.8 0.8 fusion.22
  18.7 0.1 div.24
  18.7 0.0 copy-done.2
  18.8 2.0 reduce-window.6
  20.8 0.3 slice_reduce_fusion
  21.1 0.1 bitcast_bitcast_fusion
  21.2 0.1 sqrt.12
  21.3 0.0 copy-done.5
  21.3 0.1 fusion.32
  21.5 0.0 copy-done.3
  21.5 0.0 copy-done.4
  21.5 8.6 %scatter_custom_fusion = bf16[1185,1024]{1,0:T(8,128)(2,1)} fusion(s32[784]{0:T(1024)S(1)} %get-tuple-element.8, bf16[]{:T(256)} %constant.26.clone.1, f32[1024]{0:T(1024)S(1)} %copy-done.3, f32[1024]{0:T(1024)S(1)} %copy-done.4, f32[784]{0:T(1024)S(1)} %sqrt.12, f32[784]{0:T(1024)S(1)} %div.24, bf16[784,1024]{1,0:T(8,128)(2,1)S(1)} %gather_fusion.1, ...), kind=kCustom, calls=%fused_computation.32 | custom fusion | flops 5619712 | bytes 4049922 | tf_op jit(solution)/shard_map/scatter | solution.py:45
  30.1 3.3 %slice.22 = bf16[1184,1024]{1,0:T(8,128)(2,1)} slice(bf16[1185,1024]{1,0:T(8,128)(2,1)} %scatter_custom_fusion), slice={[0:1184], [0:1024]} | slice | bytes 4849664 | tf_op jit(solution)/shard_map/slice | solution.py:43
  33.4 4.2 %reshape.103 = bf16[16,74,1024]{2,1,0:T(8,128)(2,1)} reshape(bf16[1184,1024]{1,0:T(8,128)(2,1)} %slice.22) | data formatting | bytes 4849664 | tf_op jit(solution)/shard_map/reshape | solution.py:46
  37.6 66.0 %all_to_all.10 = bf16[16,74,1024]{2,1,0:T(8,128)(2,1)} all-to-all(bf16[16,74,1024]{2,1,0:T(8,128)(2,1)} %reshape.103), channel_id=1, replica_groups=mesh['expert'=16,'dp'=2] {'expert'}, dimensions={0} | all-to-all | bytes 4849664 | tf_op jit(solution)/shard_map/all_to_all | solution.py:48
  103.6 0.0 copy-start.6
  103.6 0.0 copy-start.7
  103.6 4.3 %reshape.104 = bf16[1184,1024]{1,0:T(8,128)(2,1)} reshape(bf16[16,74,1024]{2,1,0:T(8,128)(2,1)} %all_to_all.10) | data formatting | bytes 4849664 | tf_op jit(solution)/shard_map/reshape | solution.py:50
  107.9 0.0 copy-done.6
  107.9 0.0 copy-done.7
  107.9 30.2 %add_convert_fusion = bf16[1184,1024]{1,0:T(8,128)(2,1)} fusion(bf16[1,4096,1024]{2,1,0:T(8,128)(2,1)} %param.20, bf16[1184,1024]{1,0:T(8,128)(2,1)} %reshape.104, f32[4096]{0:T(1024)S(1)} %bitcast.34, bf16[1,1024,4096]{2,1,0:T(8,128)(2,1)} %param.18, f32[1024]{0:T(1024)S(1)} %bitcast.35), kind=kOutput, calls=%fused_computation.20 | convolution fusion | flops 19915145216 | bytes 21647360 | tf_op jit(solution)/shard_map/dot_general | solution.py:11
  138.1 4.2 %reshape.105 = bf16[16,74,1024]{2,1,0:T(8,128)(2,1)} reshape(bf16[1184,1024]{1,0:T(8,128)(2,1)} %add_convert_fusion) | data formatting | bytes 4849664 | tf_op jit(solution)/shard_map/reshape | solution.py:51
  142.3 5.5 %all-to-all-start.1 = ((bf16[16,74,1024]{2,1,0:T(8,128)(2,1)}), bf16[16,74,1024]{2,1,0:T(8,128)(2,1)}, u32[]{:S(2)}, u32[]{:S(2)}) async-start(bf16[16,74,1024]{2,1,0:T(8,128)(2,1)} %reshape.105), calls=%async_computation.1 | async-start | bytes 5242880 | tf_op jit(solution)/shard_map/all_to_all | solution.py:17
  147.7 0.0 copy-done.1
  147.8 0.0 copy-done
  147.8 3.6 %fusion.30 = f32[784]{0:T(1024)S(1)} fusion(f32[1024,16]{0,1:T(8,128)S(1)} %copy-done, s32[784]{0:T(1024)S(1)} %reduce.2, f32[1024]{0:T(1024)S(1)} %copy-done.3, f32[1024]{0:T(1024)S(1)} %copy-done.4, f32[784]{0:T(1024)S(1)} %sqrt.12, f32[784]{0:T(1024)S(1)} %div.24, bf16[784,1024]{1,0:T(8,128)(2,1)S(1)} %gather_fusion.1, ...), kind=kOutput, calls=%fused_computation.37 | convolution fusion | flops 159019504 | bytes 1692688 | tf_op jit(solution)/shard_map/dot_general | solution.py:36
  151.4 54.8 %all-to-all-done.1 = bf16[16,74,1024]{2,1,0:T(8,128)(2,1)} async-done(((bf16[16,74,1024]{2,1,0:T(8,128)(2,1)}), bf16[16,74,1024]{2,1,0:T(8,128)(2,1)}, u32[]{:S(2)}, u32[]{:S(2)}) %all-to-all-start.1) | async-done | bytes 2424864 | tf_op jit(solution)/shard_map/all_to_all | solution.py:17
  206.2 2.8 %reshape.106 = bf16[1184,1024]{1,0:T(8,128)(2,1)S(1)} reshape(bf16[16,74,1024]{2,1,0:T(8,128)(2,1)} %all-to-all-done.1) | data formatting | bytes 4849664 | tf_op jit(solution)/shard_map/reshape | solution.py:52
  208.9 4.1 %gather_fusion = bf16[784,1024]{1,0:T(8,128)(2,1)} fusion(bf16[1184,1024]{1,0:T(8,128)(2,1)S(1)} %reshape.106, s32[1024]{0:T(1024)S(1)} %pad_clamp_fusion), kind=kCustom, calls=%fused_computation | custom fusion | bytes 3214400 | tf_op jit(solution)/shard_map/gather | solution.py:53
  213.0 3.2 %fusion.26 = bf16[784,1024]{1,0:T(8,128)(2,1)} fusion(bf16[784,1024]{1,0:T(8,128)(2,1)} %gather_fusion, f32[784]{0:T(1024)S(1)} %add_divide_fusion, pred[784]{0:T(1024)(128)(4,1)S(1)} %lt.29, bf16[784,1024]{1,0:T(8,128)(2,1)} %copy-done.1, pred[784]{0:T(1024)(128)(4,1)S(1)} %broadcast_in_dim.44), kind=kLoop, calls=%fused_computation.30 | loop fusion | flops 5619712 | bytes 4821600 | tf_op jit(solution)/shard_map/convert_element_type | solution.py:55
  (10 shorter events, 0.1 us)
Async XLA Ops:
  0.0 147.8 %copy-start = (f32[1024,16]{0,1:T(8,128)S(1)}, f32[1024,16]{0,1:T(8,128)}, u32[]{:S(2)}) copy-start(f32[1024,16]{0,1:T(8,128)} %param.17) | copy-start | bytes 196612
  16.6 131.1 %copy-start.1 = (bf16[784,1024]{1,0:T(8,128)(2,1)}, bf16[784,1024]{1,0:T(8,128)(2,1)S(1)}, u32[]{:S(2)}) copy-start(bf16[784,1024]{1,0:T(8,128)(2,1)S(1)} %gather_fusion.1) | copy-start | bytes 4816900
  16.6 2.1 copy-start.2
  16.7 4.7 %copy-start.5 = (s32[16]{0:T(128)S(1)}, s32[16]{0:T(128)}, u32[]{:S(2)}) copy-start(s32[16]{0:T(128)} %param.14) | copy-start | bytes 196
  16.7 4.8 %copy-start.3 = (f32[1024]{0:T(1024)S(1)}, f32[1024]{0:T(1024)}, u32[]{:S(2)}) copy-start(f32[1024]{0:T(1024)} %param.16) | copy-start | bytes 12292
  16.7 4.8 %copy-start.4 = (f32[1024]{0:T(1024)S(1)}, f32[1024]{0:T(1024)}, u32[]{:S(2)}) copy-start(f32[1024]{0:T(1024)} %param.15) | copy-start | bytes 12292
  103.6 4.3 %copy-start.6 = (f32[1,4096]{1,0:T(1,128)S(1)}, f32[1,4096]{1,0:T(1,128)}, u32[]{:S(2)}) copy-start(f32[1,4096]{1,0:T(1,128)} %param.19) | copy-start | bytes 49156
  103.6 4.3 %copy-start.7 = (f32[1,1024]{1,0:T(1,128)S(1)}, f32[1,1024]{1,0:T(1,128)}, u32[]{:S(2)}) copy-start(f32[1,1024]{1,0:T(1,128)} %param.21) | copy-start | bytes 12292
  142.3 63.9 %all-to-all-start.1 = ((bf16[16,74,1024]{2,1,0:T(8,128)(2,1)}), bf16[16,74,1024]{2,1,0:T(8,128)(2,1)}, u32[]{:S(2)}, u32[]{:S(2)}) async-start(bf16[16,74,1024]{2,1,0:T(8,128)(2,1)} %reshape.105), calls=%async_computation.1 | async-start | bytes 5242880 | tf_op jit(solution)/shard_map/all_to_all | solution.py:17
where the time goes:
time: 217 us; the launch traced here: 216 us
  blocking collectives  66 us (30%)
  waiting for transfers between devices  54.8 us (25%)
  local copies, waits for them, and re-layouts  39.1 us (18%)
  matrix products  33.8 us (16%)
  other arithmetic  16.9 us (8%)
  starting transfers between devices  5.47 us (3%)
    all_to_all x1, blocking collectives, per_device(): lax.all_to_all(outgoing, 'expert', split_axis=0, concat_axis=0, tiled=True)  66 us
    all_to_all x1, waiting for transfers between devices, send_back(): lax.all_to_all(result, 'expert', split_axis=0, concat_axis=0, tiled=True)  54.8 us
    dot_general x1, matrix products, expert_rows(): jnp.dot(act, w_out[0], preferred_element_type=jnp.float32) + b_out[0]  30.2 us
    gather x3, local copies, waits for them, and re-layouts, per_device(): jnp.take_along_axis(patches, visible[:, :, None], axis=1).reshape(-1, width)  15.6 us
    scatter x1, other arithmetic, per_device(): outgoing = jnp.zeros((experts * slots + 1, width), jnp.bfloat16).at[dest]...  8.57 us
    all_to_all x1, starting transfers between devices, send_back(): lax.all_to_all(result, 'expert', split_axis=0, concat_axis=0, tiled=True)  5.47 us
  transfers between devices with their start and end apart: 1, of which 1 were waited for; matrix products, arithmetic and copies ran while one was open for 2% of the time, Pallas kernels for 0%

commit v1 on v0

v1 whole, which is shorter than its diff:
```python
import functools

import jax
import jax.numpy as jnp
from jax import lax
from jax.experimental import pallas as pl
from jax.experimental.pallas import tpu as pltpu
from jax.sharding import PartitionSpec as P

F32 = jnp.float32
BF16 = jnp.bfloat16
ANY = pl.BlockSpec(memory_space=pl.ANY)
VMEM = pl.BlockSpec(memory_space=pltpu.VMEM)
VMEM_LIMIT = 60 * 1024 * 1024


def ceil_to(value, unit):
    return -(-value // unit) * unit


def largest_tile(total, limit, unit):
    for tile in range(limit // unit * unit, 0, -unit):
        if total % tile == 0:
            return tile
    return total


def dispatch_kernel(
    stride, patches, wanted, col, col_x, row, row_x, cap_row, cap_col, gain, bias, router,
    x_out, gate_out, dest_out, outgoing, patch_buf, pick, xs, hb, sems,
):
    tokens, width = xs.shape
    experts = router.shape[1]
    slots_all = outgoing.shape[0]

    part = largest_tile(width, 256, 128)

    def load(i):
        at = pl.ds(i * part, part)
        return pltpu.make_async_copy(patches.at[:, at], patch_buf.at[:, at], sems.at[i])

    for i in range(width // part):
        load(i).start()

    chunk = largest_tile(tokens, 128, 16)
    lane = lax.broadcasted_iota(jnp.int32, (chunk, patches.shape[0]), 1)

    @pl.loop(0, tokens // chunk)
    def _(c):
        at = pl.ds(pl.multiple_of(c * chunk, chunk), chunk)
        pick[at, :] = jnp.where(wanted[at, :] == lane, 1.0, 0.0).astype(BF16)

    tri_r = lax.broadcasted_iota(jnp.int32, (tokens, tokens), 0)
    tri_c = lax.broadcasted_iota(jnp.int32, (tokens, tokens), 1)
    hot_row = jnp.where(
        row[...] == lax.broadcasted_iota(jnp.int32, (experts, tokens), 0), 1.0, 0.0
    )
    before_row = jnp.dot(
        hot_row.astype(BF16), jnp.where(tri_r < tri_c, 1.0, 0.0).astype(BF16),
        preferred_element_type=F32,
    )
    rank_row = jnp.sum(before_row * hot_row, axis=0, keepdims=True).astype(jnp.int32)
    limit_row = jnp.sum(
        hot_row * cap_col[...].astype(F32), axis=0, keepdims=True
    ).astype(jnp.int32)
    dest_row = jnp.where(rank_row < limit_row, row_x[...] * stride + rank_row, -1)

    hot_col = jnp.where(
        col[...] == lax.broadcasted_iota(jnp.int32, (tokens, experts), 1), 1.0, 0.0
    )
    before_col = jnp.dot(
        jnp.where(tri_c < tri_r, 1.0, 0.0).astype(BF16), hot_col.astype(BF16),
        preferred_element_type=F32,
    )
    rank_col = jnp.sum(before_col * hot_col, axis=1, keepdims=True).astype(jnp.int32)
    limit_col = jnp.sum(
        hot_col * cap_row[...].astype(F32), axis=1, keepdims=True
    ).astype(jnp.int32)
    dest_out[...] = jnp.where(rank_col < limit_col, col_x[...] * stride + rank_col, -1)

    for i in range(width // part):
        load(i).wait()
        at = pl.ds(i * part, part)
        xs[:, at] = jnp.dot(pick[...], patch_buf[:, at], preferred_element_type=F32)

    for c in range(tokens // chunk):
        at = pl.ds(c * chunk, chunk)
        xf = xs[at, :]
        mean = jnp.mean(xf, axis=1, keepdims=True)
        off = xf - mean
        var = jnp.mean(off * off, axis=1, keepdims=True)
        h = off / jnp.sqrt(var + 1e-06) * gain[...] + bias[...]
        hb[at, :] = h.astype(BF16)
        x_out[at, :] = xf.astype(BF16)
        logits = jnp.dot(h, router[...], precision=lax.Precision.HIGHEST)
        picked_logit = jnp.sum(
            logits * hot_col[c * chunk : (c + 1) * chunk], axis=1, keepdims=True
        )
        gate_out[at, :] = jax.nn.sigmoid(picked_logit)

    step = largest_tile(slots_all, 256, 16)
    slot = lax.broadcasted_iota(jnp.int32, (step, tokens), 0)

    @pl.loop(0, slots_all // step)
    def _(s):
        place = jnp.where(dest_row - s * step == slot, 1.0, 0.0).astype(BF16)
        at = pl.ds(pl.multiple_of(s * step, step), step)
        outgoing[at, :] = jnp.dot(place, hb[...], preferred_element_type=F32).astype(BF16)


def partner_of(me, k):
    bit = 1
    result = me
    while bit <= k:
        if k & bit:
            result = result + bit * (1 - 2 * lax.rem(lax.div(me, bit), 2))
        bit *= 2
    return result


def expert_kernel(
    devices, stride, outgoing, w_in, b_in, w_out, b_out, back, recv, res, act, w1, w2,
    send_sem, recv_sem, bsend_sem, brecv_sem, w_sem,
):
    me = lax.axis_index("expert")
    hidden = w1.shape[1]
    width = w1.shape[0]
    load_1 = pltpu.make_async_copy(w_in.at[0], w1, w_sem.at[0])
    load_2 = pltpu.make_async_copy(w_out.at[0], w2, w_sem.at[1])
    own_in = pltpu.make_async_copy(
        outgoing.at[pl.ds(0, stride)], recv.at[pl.ds(0, stride)], w_sem.at[2]
    )
    own_in.start()
    load_1.start()
    load_2.start()

    barrier = pltpu.get_barrier_semaphore()
    for k in range(1, devices):
        pl.semaphore_signal(
            barrier, inc=1, device_id={"expert": partner_of(me, k)},
            device_id_type=pl.DeviceIdType.MESH,
        )
    pl.semaphore_wait(barrier, devices - 1)

    def forward(k):
        at = pl.ds(k * stride, stride)
        return pltpu.make_async_remote_copy(
            src_ref=outgoing.at[at], dst_ref=recv.at[at], send_sem=send_sem.at[k],
            recv_sem=recv_sem.at[k], device_id={"expert": partner_of(me, k)},
            device_id_type=pl.DeviceIdType.MESH,
        )

    def backward(k):
        at = pl.ds(k * stride, stride)
        return pltpu.make_async_remote_copy(
            src_ref=res.at[at], dst_ref=back.at[at], send_sem=bsend_sem.at[k],
            recv_sem=brecv_sem.at[k], device_id={"expert": partner_of(me, k)},
            device_id_type=pl.DeviceIdType.MESH,
        )

    groups = 4 if devices % 4 == 0 else 1
    size = devices // groups
    send_order = (2, 3, 1, 0) if groups == 4 else (0,)
    work_order = (0, 2, 3, 1) if groups == 4 else (0,)
    for g in send_order:
        for k in range(g * size, (g + 1) * size):
            if k:
                forward(k).start()

    rows = size * stride
    tile_f = largest_tile(hidden, 512, 128)
    tile_d = largest_tile(width, 256, 128)
    own_out = pltpu.make_async_copy(
        res.at[pl.ds(0, stride)], back.at[pl.ds(0, stride)], w_sem.at[3]
    )
    for turn, g in enumerate(work_order):
        for k in range(g * size, (g + 1) * size):
            if k:
                forward(k).wait_recv()
            else:
                own_in.wait()
        base = g * rows
        if turn == 0:
            load_1.wait()

        @pl.loop(0, hidden // tile_f)
        def _(f):
            at = pl.ds(pl.multiple_of(f * tile_f, tile_f), tile_f)
            v = jnp.dot(
                recv[base : base + rows, :], w1[:, at], preferred_element_type=F32
            ) + b_in[:, at]
            act[:, at] = jax.nn.gelu(v, approximate=True).astype(BF16)

        if turn == 0:
            load_2.wait()

        @pl.loop(0, width // tile_d)
        def _(d):
            at = pl.ds(pl.multiple_of(d * tile_d, tile_d), tile_d)
            v = jnp.dot(act[...], w2[:, at], preferred_element_type=F32) + b_out[:, at]
            res[base : base + rows, at] = v.astype(BF16)

        for k in range(g * size, (g + 1) * size):
            if k:
                backward(k).start()
            else:
                own_out.start()

    for k in range(1, devices):
        forward(k).wait_send()
    own_out.wait()
    for k in range(1, devices):
        backward(k).wait()


def combine_kernel(x, gate, dest, back, out):
    slots_all = back.shape[0]
    rows = x.shape[0]
    slot = lax.broadcasted_iota(jnp.int32, (rows, slots_all), 1)
    place = jnp.where(dest[...] == slot, 1.0, 0.0).astype(BF16)
    picked = jnp.dot(place, back[...], preferred_element_type=F32)
    out[...] = (x[...].astype(F32) + gate[...] * picked).astype(BF16)


def per_device(
    patches, visible, routes, expert_cap, norm_gain, norm_bias, router, w_in, b_in, w_out, b_out
):
    images, count, width = patches.shape
    keep = visible.shape[1]
    devices = lax.axis_size("expert")
    experts = expert_cap.shape[0]
    hidden = w_in.shape[2]
    tokens = images * keep
    slots = max(2, (3 * tokens + 2 * experts - 1) // (2 * experts))
    stride = ceil_to(slots, 16)
    total = experts * stride
    me = lax.axis_index("expert").astype(jnp.int32)

    wanted = (visible * images + jnp.arange(images, dtype=jnp.int32)[:, None]).reshape(tokens, 1)
    row = routes.reshape(1, tokens)
    x, gate, dest, outgoing = pl.pallas_call(
        functools.partial(dispatch_kernel, stride),
        out_shape=(
            jax.ShapeDtypeStruct((tokens, width), BF16),
            jax.ShapeDtypeStruct((tokens, 1), F32),
            jax.ShapeDtypeStruct((tokens, 1), jnp.int32),
            jax.ShapeDtypeStruct((total, width), BF16),
        ),
        in_specs=[ANY] + [VMEM] * 10,
        out_specs=(VMEM,) * 4,
        scratch_shapes=[
            pltpu.VMEM((count * images, width), BF16),
            pltpu.VMEM((tokens, count * images), BF16),
            pltpu.VMEM((tokens, width), F32),
            pltpu.VMEM((tokens, width), BF16),
            pltpu.SemaphoreType.DMA((width // largest_tile(width, 256, 128),)),
        ],
        compiler_params=pltpu.CompilerParams(vmem_limit_bytes=VMEM_LIMIT),
        name="dispatch",
    )(
        patches.transpose(1, 0, 2).reshape(count * images, width), wanted, routes, routes ^ me, row, row ^ me,
        expert_cap.reshape(1, experts), expert_cap.reshape(experts, 1),
        norm_gain.reshape(1, width), norm_bias.reshape(1, width), router,
    )

    group = devices // 4 if devices % 4 == 0 else devices
    back = pl.pallas_call(
        functools.partial(expert_kernel, devices, stride),
        out_shape=jax.ShapeDtypeStruct((total, width), BF16),
        in_specs=[ANY, ANY, VMEM, ANY, VMEM],
        out_specs=ANY,
        scratch_shapes=[
            pltpu.VMEM((total, width), BF16),
            pltpu.VMEM((total, width), BF16),
            pltpu.VMEM((group * stride, hidden), BF16),
            pltpu.VMEM((width, hidden), BF16),
            pltpu.VMEM((hidden, width), BF16),
            pltpu.SemaphoreType.DMA((devices,)),
            pltpu.SemaphoreType.DMA((devices,)),
            pltpu.SemaphoreType.DMA((devices,)),
            pltpu.SemaphoreType.DMA((devices,)),
            pltpu.SemaphoreType.DMA((4,)),
        ],
        compiler_params=pltpu.CompilerParams(
            collective_id=0, has_side_effects=True, vmem_limit_bytes=VMEM_LIMIT
        ),
        name="experts",
    )(outgoing, w_in, b_in, w_out, b_out)

    rows = largest_tile(tokens, 256, 16)
    return pl.pallas_call(
        combine_kernel,
        grid=(tokens // rows,),
        out_shape=jax.ShapeDtypeStruct((tokens, width), BF16),
        in_specs=[
            pl.BlockSpec((rows, width), lambda i: (i, 0)),
            pl.BlockSpec((rows, 1), lambda i: (i, 0)),
            pl.BlockSpec((rows, 1), lambda i: (i, 0)),
            pl.BlockSpec((total, width), lambda i: (0, 0)),
        ],
        out_specs=pl.BlockSpec((rows, width), lambda i: (i, 0)),
        compiler_params=pltpu.CompilerParams(vmem_limit_bytes=VMEM_LIMIT),
        name="combine",
    )(x, gate, dest, back)


def solution(mesh):
    return jax.shard_map(
        per_device,
        mesh=mesh,
        in_specs=(
            P(("dp", "expert"), None, None),
            P(("dp", "expert"), None),
            P(("dp", "expert"), None),
            P("dp"),
            P(),
            P(),
            P(),
            P("expert", None, None),
            P("expert", None),
            P("expert", None, None),
            P("expert", None),
        ),
        out_specs=P(("dp", "expert"), None),
        check_vma=False,
    )
```

time: 217 us -> 172 us (0.79)
  the two profiles are of different devices: /device:TPU:12 before, /device:TPU:0 now
where the time goes in v1:
time: 172 us
  Pallas kernels  164 us (95%)
  local copies, waits for them, and re-layouts  4.94 us (3%)
  other arithmetic  2.83 us (2%)
    pallas_call x1, Pallas kernels, per_device(): pl.pallas_call(functools.partial(expert_kernel, devices, stride), out_sha...  131 us
    pallas_call x1, Pallas kernels, per_device(): pl.pallas_call(functools.partial(dispatch_kernel, stride), out_shape=(jax...  25.1 us
    pallas_call x1, Pallas kernels, per_device(): pl.pallas_call(combine_kernel, grid=(tokens // rows,), out_shape=jax.Shap...  8.32 us

profile of v1, /device:TPU:0, one launch (start us, length us, event | category | flops | bytes accessed | tf_op | source)
XLA Modules:
  0.0 171.9 jit_solution(4916904110303456321)
XLA Ops:
  0.0 1.3 broadcast_xor_fusion.1.row_x
  1.3 0.7 iota_add_fusion
  2.0 1.3 copy.25.cap_col
  3.3 0.9 reshape.40.wanted
  4.2 0.9 copy.24.col
  5.1 0.0 copy-start
  5.1 0.8 broadcast_xor_fusion.col_x
  6.0 1.8 %copy.26.router = f32[1024,16]{1,0:T(8,128)} copy(f32[1024,16]{0,1:T(8,128)} %param.17) | data formatting | bytes 131072 | tf_op args[6]
  7.8 0.0 copy-done
  7.8 25.1 %dispatch.1 = (bf16[784,1024]{1,0:T(8,128)(2,1)}, f32[784,1]{1,0:T(8,128)}, s32[784,1]{1,0:T(8,128)}, bf16[1280,1024]{1,0:T(8,128)(2,1)}) custom-call(bf16[3136,1024]{1,0:T(8,128)(2,1)} %bitcast.9, s32[784,1]{1,0:T(8,128)} %reshape.40.wanted, s32[784,1]{1,0:T(8,128)} %copy-done, s32[784,1]{1,0:T(8,128)} %broadcast_xor_fusion.col_x, s32[1,784]{1,0:T(1,128)} %bitcast.10, ...), custom_call_target="tpu_custom_call" | custom-call | tf_op jit(solution)/shard_map/dispatch/pallas_call | solution.py:241
  32.9 130.7 %experts.1.back = bf16[1280,1024]{1,0:T(8,128)(2,1)} custom-call(bf16[1280,1024]{1,0:T(8,128)(2,1)} %get-tuple-element.12.outgoing, bf16[1,1024,4096]{2,1,0:T(8,128)(2,1)} %w_in.1, f32[1,4096]{1,0:T(1,128)} %b_in.1, bf16[1,4096,1024]{2,1,0:T(8,128)(2,1)} %w_out.1, f32[1,1024]{1,0:T(1,128)} %b_out.1), custom_call_target="tpu_custom_call" | custom-call | tf_op jit(solution)/shard_map/experts/pallas_call | solution.py:267
  163.6 8.3 %combine.1 = bf16[784,1024]{1,0:T(8,128)(2,1)} custom-call(bf16[784,1024]{1,0:T(8,128)(2,1)} %get-tuple-element.9.x, f32[784,1]{1,0:T(8,128)} %get-tuple-element.10.gate, s32[784,1]{1,0:T(8,128)} %get-tuple-element.11.dest, bf16[1280,1024]{1,0:T(8,128)(2,1)} %experts.1.back), custom_call_target="tpu_custom_call" | custom-call | tf_op jit(solution)/shard_map/combine/pallas_call | solution.py:291
Async XLA Ops:
  5.1 2.7 %copy-start = (s32[784,1]{1,0:T(8,128)}, s32[784,1]{1,0:T(8,128)S(1)}, u32[]{:S(2)}) copy-start(s32[784,1]{1,0:T(8,128)S(1)} %copy.24.col) | copy-start | bytes 9412

commit v2 on v1

--- a/solution.py
+++ b/solution.py
@@ -26,12 +26,13 @@
 
 
 def dispatch_kernel(
-    stride, patches, wanted, col, col_x, row, row_x, cap_row, cap_col, gain, bias, router,
+    stride, patches, wanted, row, cap, gain, bias, router_t,
     x_out, gate_out, dest_out, outgoing, patch_buf, pick, xs, hb, sems,
 ):
     tokens, width = xs.shape
-    experts = router.shape[1]
+    experts = router_t.shape[0]
     slots_all = outgoing.shape[0]
+    me = lax.axis_index("expert")
 
     part = largest_tile(width, 256, 128)
 
@@ -52,31 +53,30 @@
 
     tri_r = lax.broadcasted_iota(jnp.int32, (tokens, tokens), 0)
     tri_c = lax.broadcasted_iota(jnp.int32, (tokens, tokens), 1)
-    hot_row = jnp.where(
-        row[...] == lax.broadcasted_iota(jnp.int32, (experts, tokens), 0), 1.0, 0.0
-    )
-    before_row = jnp.dot(
+    chosen = row[...]
+    hot_row = jnp.where(chosen == lax.broadcasted_iota(jnp.int32, (experts, tokens), 0), 1.0, 0.0)
+    before = jnp.dot(
         hot_row.astype(BF16), jnp.where(tri_r < tri_c, 1.0, 0.0).astype(BF16),
         preferred_element_type=F32,
     )
-    rank_row = jnp.sum(before_row * hot_row, axis=0, keepdims=True).astype(jnp.int32)
-    limit_row = jnp.sum(
-        hot_row * cap_col[...].astype(F32), axis=0, keepdims=True
+    rank = jnp.sum(before * hot_row, axis=0, keepdims=True).astype(jnp.int32)
+    caps = jnp.broadcast_to(cap[...].astype(F32), (8, experts))
+    limit = jnp.dot(caps, hot_row, precision=lax.Precision.HIGHEST)[0:1]
+    dest_row = jnp.where(rank < limit.astype(jnp.int32), (chosen ^ me) * stride + rank, -1)
+
+    digit = lax.broadcasted_iota(jnp.int32, (8, tokens), 0)
+    full = dest_row + 1
+    digits = jnp.where(
+        digit == 0, full >> 7, jnp.where(digit == 1, full & 127, jnp.where(digit == 2, chosen, 0))
+    )
+    columns = lax.dot_general(
+        jnp.where(tri_r == tri_c, 1.0, 0.0).astype(BF16), digits.astype(F32).astype(BF16),
+        (((1,), (1,)), ((), ())), preferred_element_type=F32,
     ).astype(jnp.int32)
-    dest_row = jnp.where(rank_row < limit_row, row_x[...] * stride + rank_row, -1)
-
+    dest_out[...] = columns[:, 0:1] * 128 + columns[:, 1:2] - 1
     hot_col = jnp.where(
-        col[...] == lax.broadcasted_iota(jnp.int32, (tokens, experts), 1), 1.0, 0.0
-    )
-    before_col = jnp.dot(
-        jnp.where(tri_c < tri_r, 1.0, 0.0).astype(BF16), hot_col.astype(BF16),
-        preferred_element_type=F32,
-    )
-    rank_col = jnp.sum(before_col * hot_col, axis=1, keepdims=True).astype(jnp.int32)
-    limit_col = jnp.sum(
-        hot_col * cap_row[...].astype(F32), axis=1, keepdims=True
-    ).astype(jnp.int32)
-    dest_out[...] = jnp.where(rank_col < limit_col, col_x[...] * stride + rank_col, -1)
+        columns[:, 2:3] == lax.broadcasted_iota(jnp.int32, (tokens, experts), 1), 1.0, 0.0
+    )
 
     for i in range(width // part):
         load(i).wait()
@@ -92,7 +92,10 @@
         h = off / jnp.sqrt(var + 1e-06) * gain[...] + bias[...]
         hb[at, :] = h.astype(BF16)
         x_out[at, :] = xf.astype(BF16)
-        logits = jnp.dot(h, router[...], precision=lax.Precision.HIGHEST)
+        logits = lax.dot_general(
+            h, router_t[...], (((1,), (1,)), ((), ())), precision=lax.Precision.HIGHEST,
+            preferred_element_type=F32,
+        )
         picked_logit = jnp.sum(
             logits * hot_col[c * chunk : (c + 1) * chunk], axis=1, keepdims=True
         )
@@ -119,7 +122,7 @@
 
 
 def expert_kernel(
-    devices, stride, outgoing, w_in, b_in, w_out, b_out, back, recv, res, act, w1, w2,
+    devices, stride, slots, outgoing, w_in, b_in, w_out, b_out, back, recv, res, act, w1, w2,
     send_sem, recv_sem, bsend_sem, brecv_sem, w_sem,
 ):
     me = lax.axis_index("expert")
@@ -127,6 +130,8 @@
     width = w1.shape[0]
     load_1 = pltpu.make_async_copy(w_in.at[0], w1, w_sem.at[0])
     load_2 = pltpu.make_async_copy(w_out.at[0], w2, w_sem.at[1])
+    if slots < stride:
+        recv[...] = jnp.zeros_like(recv)
     own_in = pltpu.make_async_copy(
         outgoing.at[pl.ds(0, stride)], recv.at[pl.ds(0, stride)], w_sem.at[2]
     )
@@ -143,7 +148,7 @@
     pl.semaphore_wait(barrier, devices - 1)
 
     def forward(k):
-        at = pl.ds(k * stride, stride)
+        at = pl.ds(k * stride, slots)
         return pltpu.make_async_remote_copy(
             src_ref=outgoing.at[at], dst_ref=recv.at[at], send_sem=send_sem.at[k],
             recv_sem=recv_sem.at[k], device_id={"expert": partner_of(me, k)},
@@ -151,7 +156,7 @@
         )
 
     def backward(k):
-        at = pl.ds(k * stride, stride)
+        at = pl.ds(k * stride, slots)
         return pltpu.make_async_remote_copy(
             src_ref=res.at[at], dst_ref=back.at[at], send_sem=bsend_sem.at[k],
             recv_sem=brecv_sem.at[k], device_id={"expert": partner_of(me, k)},
@@ -161,7 +166,7 @@
     groups = 4 if devices % 4 == 0 else 1
     size = devices // groups
     send_order = (2, 3, 1, 0) if groups == 4 else (0,)
-    work_order = (0, 2, 3, 1) if groups == 4 else (0,)
+    work_order = (0, 2, 1, 3) if groups == 4 else (0,)
     for g in send_order:
         for k in range(g * size, (g + 1) * size):
             if k:
@@ -213,12 +218,23 @@
         backward(k).wait()
 
 
-def combine_kernel(x, gate, dest, back, out):
+def combine_kernel(stride, slots, x, gate, dest, back, out, place):
     slots_all = back.shape[0]
     rows = x.shape[0]
-    slot = lax.broadcasted_iota(jnp.int32, (rows, slots_all), 1)
-    place = jnp.where(dest[...] == slot, 1.0, 0.0).astype(BF16)
-    picked = jnp.dot(place, back[...], preferred_element_type=F32)
+    chunk = largest_tile(rows, 128, 16)
+
+    @pl.when(pl.program_id(0) == 0)
+    def _():
+        slot = lax.broadcasted_iota(jnp.int32, (chunk, slots_all), 1)
+
+        @pl.loop(0, rows // chunk)
+        def _(c):
+            at = pl.ds(pl.multiple_of(c * chunk, chunk), chunk)
+            place[at, :] = jnp.where(dest[at, :] == slot, 1.0, 0.0).astype(BF16)
+
+    used = lax.rem(lax.broadcasted_iota(jnp.int32, back.shape, 0), stride) < slots
+    result = jnp.where(used, back[...], jnp.zeros((), BF16))
+    picked = jnp.dot(place[...], result, preferred_element_type=F32)
     out[...] = (x[...].astype(F32) + gate[...] * picked).astype(BF16)
 
 
@@ -234,7 +250,6 @@
     slots = max(2, (3 * tokens + 2 * experts - 1) // (2 * experts))
     stride = ceil_to(slots, 16)
     total = experts * stride
-    me = lax.axis_index("expert").astype(jnp.int32)
 
     wanted = (visible * images + jnp.arange(images, dtype=jnp.int32)[:, None]).reshape(tokens, 1)
     row = routes.reshape(1, tokens)
@@ -246,7 +261,7 @@
             jax.ShapeDtypeStruct((tokens, 1), jnp.int32),
             jax.ShapeDtypeStruct((total, width), BF16),
         ),
-        in_specs=[ANY] + [VMEM] * 10,
+        in_specs=[ANY] + [VMEM] * 6,
         out_specs=(VMEM,) * 4,
         scratch_shapes=[
             pltpu.VMEM((count * images, width), BF16),
@@ -258,14 +273,15 @@
         compiler_params=pltpu.CompilerParams(vmem_limit_bytes=VMEM_LIMIT),
         name="dispatch",
     )(
-        patches.transpose(1, 0, 2).reshape(count * images, width), wanted, routes, routes ^ me, row, row ^ me,
-        expert_cap.reshape(1, experts), expert_cap.reshape(experts, 1),
-        norm_gain.reshape(1, width), norm_bias.reshape(1, width), router,
-    )
-
+        patches.transpose(1, 0, 2).reshape(count * images, width), wanted, row,
+        expert_cap.reshape(1, experts),
+        norm_gain.reshape(1, width), norm_bias.reshape(1, width), router.T,
+    )
+
+    sent = ceil_to(slots, 8)
     group = devices // 4 if devices % 4 == 0 else devices
     back = pl.pallas_call(
-        functools.partial(expert_kernel, devices, stride),
+        functools.partial(expert_kernel, devices, stride, sent),
         out_shape=jax.ShapeDtypeStruct((total, width), BF16),
         in_specs=[ANY, ANY, VMEM, ANY, VMEM],
         out_specs=ANY,
@@ -287,18 +303,19 @@
         name="experts",
     )(outgoing, w_in, b_in, w_out, b_out)
 
-    rows = largest_tile(tokens, 256, 16)
+    tile = largest_tile(width, 256, 128)
     return pl.pallas_call(
-        combine_kernel,
-        grid=(tokens // rows,),
+        functools.partial(combine_kernel, stride, slots),
+        grid=(width // tile,),
         out_shape=jax.ShapeDtypeStruct((tokens, width), BF16),
         in_specs=[
-            pl.BlockSpec((rows, width), lambda i: (i, 0)),
-            pl.BlockSpec((rows, 1), lambda i: (i, 0)),
-            pl.BlockSpec((rows, 1), lambda i: (i, 0)),
-            pl.BlockSpec((total, width), lambda i: (0, 0)),
+            pl.BlockSpec((tokens, tile), lambda i: (0, i)),
+            pl.BlockSpec((tokens, 1), lambda i: (0, 0)),
+            pl.BlockSpec((tokens, 1), lambda i: (0, 0)),
+            pl.BlockSpec((total, tile), lambda i: (0, i)),
         ],
-        out_specs=pl.BlockSpec((rows, width), lambda i: (i, 0)),
+        out_specs=pl.BlockSpec((tokens, tile), lambda i: (0, i)),
+        scratch_shapes=[pltpu.VMEM((tokens, total), BF16)],
         compiler_params=pltpu.CompilerParams(vmem_limit_bytes=VMEM_LIMIT),
         name="combine",
     )(x, gate, dest, back)

time: 172 us -> 155 us (0.901)
  the two profiles are of different devices: /device:TPU:0 before, /device:TPU:12 now
where the time goes in v2:
time: 155 us
  Pallas kernels  153 us (99%)
    pallas_call x1, Pallas kernels, per_device(): pl.pallas_call(functools.partial(expert_kernel, devices, stride, sent), o...  122 us
    pallas_call x1, Pallas kernels, per_device(): pl.pallas_call(functools.partial(dispatch_kernel, stride), out_shape=(jax...  24 us
    pallas_call x1, Pallas kernels, per_device(): pl.pallas_call(functools.partial(combine_kernel, stride, slots), grid=(wi...  6.78 us

profile of v2, /device:TPU:12, one launch (start us, length us, event | category | flops | bytes accessed | tf_op | source)
XLA Modules:
  0.0 154.6 jit_solution(2330443594256979131)
XLA Ops:
  0.0 0.7 iota_add_fusion
  0.7 0.9 reshape.24.wanted
  1.6 24.0 %dispatch.1 = (bf16[784,1024]{1,0:T(8,128)(2,1)}, f32[784,1]{1,0:T(8,128)}, s32[784,1]{1,0:T(8,128)}, bf16[1280,1024]{1,0:T(8,128)(2,1)}) custom-call(bf16[3136,1024]{1,0:T(8,128)(2,1)} %bitcast.8, s32[784,1]{1,0:T(8,128)} %reshape.24.wanted, s32[1,784]{1,0:T(1,128)} %bitcast.12, s32[1,16]{1,0:T(1,128)} %bitcast.13, f32[1,1024]{1,0:T(1,128)} %bitcast.10, ...), custom_call_target="tpu_custom_call" | custom-call | tf_op jit(solution)/shard_map/dispatch/pallas_call | solution.py:256
  25.6 122.2 %experts.1.back = bf16[1280,1024]{1,0:T(8,128)(2,1)} custom-call(bf16[1280,1024]{1,0:T(8,128)(2,1)} %get-tuple-element.12.outgoing, bf16[1,1024,4096]{2,1,0:T(8,128)(2,1)} %w_in.1, f32[1,4096]{1,0:T(1,128)} %b_in.1, bf16[1,4096,1024]{2,1,0:T(8,128)(2,1)} %w_out.1, f32[1,1024]{1,0:T(1,128)} %b_out.1), custom_call_target="tpu_custom_call" | custom-call | tf_op jit(solution)/shard_map/experts/pallas_call | solution.py:283
  147.8 6.8 %combine.1 = bf16[784,1024]{1,0:T(8,128)(2,1)} custom-call(bf16[784,1024]{1,0:T(8,128)(2,1)} %get-tuple-element.9.x, f32[784,1]{1,0:T(8,128)} %get-tuple-element.10.gate, s32[784,1]{1,0:T(8,128)} %get-tuple-element.11.dest, bf16[1280,1024]{1,0:T(8,128)(2,1)} %experts.1.back), custom_call_target="tpu_custom_call" | custom-call | tf_op jit(solution)/shard_map/combine/pallas_call | solution.py:307
